TPU v7x, 32 devices: a 4x2x2 block of a 4x4x8 slice. The times are simulated.
32 devices in a mesh: data: 4 (over y, z), stage: 8 (over x, core).
Axes of the slice: x: 4, y: 2, z: 2, core: 2. Of those that a mesh axis runs over, the one named last changes fastest.
The devices are a block of a 4x4x8 slice.
Arguments:
- x_init: float32 [4, 256, 16], P('data'), parts along dimension 0
- w_in: bfloat16 [16, 384], replicated
- w_out: bfloat16 [384, 16], replicated
- w_qkv: bfloat16 [8, 384, 1152], P('stage')
- w_proj: bfloat16 [8, 6, 64, 384], P('stage')
- w_up: bfloat16 [8, 384, 1536], P('stage')
- w_down: bfloat16 [8, 1536, 384], P('stage')
- mod_table: float32 [32, 8, 6, 384], P(None, 'stage')
- coef_keep: float32 [32], replicated
- coef_noise: float32 [32], replicated
- h_warm: bfloat16 [2, 7, 4, 256, 384], P(None, None, 'data'), parts along dimension 2
Outputs:
- output: float32 [4, 256, 16], P('data'), parts along dimension 0
There are 4 independent parts. A program takes and returns all parts, laid end to end along the dimension named above; an argument that names none is the same for every part.
All inputs are finite; a program needn't handle non-finite values.
Results may differ from a plain program's by a relative error of at most 0.0112909.
Values are sent between devices in bfloat16 or wider.
A program may use at most 768 MiB of HBM per device.

v0:
```python
import jax
import jax.numpy as jnp
from jax import lax
from jax.sharding import PartitionSpec as P

LN_EPS = 1e-6


def layer_norm(hidden):
    row_mean = jnp.mean(hidden, axis=-1, keepdims=True)
    centered = hidden - row_mean
    row_var = jnp.mean(centered * centered, axis=-1, keepdims=True)
    return centered * lax.rsqrt(row_var + LN_EPS)


def local_block(hidden, w_qkv_l, w_proj_l, w_up_l, w_down_l, mod_l):
    batch_rows, tokens, model_width = hidden.shape
    num_heads = w_proj_l.shape[0]
    head_dim = w_proj_l.shape[1]
    normed = (layer_norm(hidden) * (1.0 + mod_l[1]) + mod_l[0]).astype(jnp.bfloat16)
    qkv_all = jnp.einsum('bnd,de->bne', normed, w_qkv_l, preferred_element_type=jnp.float32).astype(jnp.bfloat16)
    qkv_all = qkv_all.reshape(batch_rows, tokens, 3, num_heads, head_dim)
    scores = jnp.einsum('bqhd,bkhd->bhqk', qkv_all[:, :, 0], qkv_all[:, :, 1], preferred_element_type=jnp.float32) * head_dim ** -0.5
    attn_prob = jax.nn.softmax(scores, axis=-1).astype(jnp.bfloat16)
    attn_out = jnp.einsum('bhqk,bkhd->bqhd', attn_prob, qkv_all[:, :, 2], preferred_element_type=jnp.float32).astype(jnp.bfloat16)
    hidden = hidden + mod_l[2] * jnp.einsum('bqhd,hde->bqe', attn_out, w_proj_l, preferred_element_type=jnp.float32)
    normed = (layer_norm(hidden) * (1.0 + mod_l[4]) + mod_l[3]).astype(jnp.bfloat16)
    mlp_act = jax.nn.gelu(jnp.einsum('bnd,df->bnf', normed, w_up_l, preferred_element_type=jnp.float32)).astype(jnp.bfloat16)
    return hidden + mod_l[5] * jnp.einsum('bnf,fd->bnd', mlp_act, w_down_l, preferred_element_type=jnp.float32)


def solution(mesh):
    stages = mesh.shape['stage']
    fwd_pairs = [(src_idx, src_idx + 1) for src_idx in range(stages - 1)]
    back_pairs = [(stages - 1, 0)]

    def shard_body(x_init, w_in, w_out, w_qkv, w_proj, w_up, w_down, mod_table, coef_keep, coef_noise, h_warm):
        stage_idx = lax.axis_index('stage')
        is_first = stage_idx == 0
        is_last = stage_idx == stages - 1
        num_steps = coef_keep.shape[0]
        blocks = w_qkv.shape[0]
        warm_pair = lax.dynamic_index_in_dim(h_warm, jnp.maximum(stage_idx - 1, 0), 1, keepdims=False)

        def one_step(step_idx, loop_state):
            bound_now, bound_next, lat_now, x_cur = loop_state
            embedded = jnp.einsum('rnc,cd->rnd', lat_now.astype(jnp.bfloat16), w_in, preferred_element_type=jnp.float32)
            hidden = jnp.where(is_first, embedded, bound_now.astype(jnp.float32))
            mod_step = mod_table[step_idx]
            for blk_idx in range(blocks):
                hidden = local_block(hidden, w_qkv[blk_idx], w_proj[blk_idx], w_up[blk_idx], w_down[blk_idx], mod_step[blk_idx])
            normed = layer_norm(hidden).astype(jnp.bfloat16)
            noise_pred = jnp.einsum('rnd,dc->rnc', normed, w_out, preferred_element_type=jnp.float32)
            x_next = coef_keep[step_idx] * x_cur + coef_noise[step_idx] * noise_pred
            sent_bound = lax.ppermute(hidden.astype(jnp.bfloat16), 'stage', fwd_pairs)
            lat_recv = lax.ppermute(x_next, 'stage', back_pairs)
            x_new = jnp.where(is_first, lat_recv, x_next)
            return (bound_next, sent_bound, x_cur, x_new)

        init_state = (warm_pair[0], warm_pair[1], x_init, x_init)
        final_state = lax.fori_loop(0, num_steps, one_step, init_state)
        x_last = jnp.where(is_last, final_state[3], jnp.zeros_like(final_state[3]))
        return lax.psum(x_last, 'stage')

    return jax.shard_map(
        shard_body,
        mesh=mesh,
        in_specs=(P('data'), P(), P(), P('stage'), P('stage'), P('stage'), P('stage'), P(None, 'stage'), P(), P(), P(None, None, 'data')),
        out_specs=P('data'),
        check_vma=False,
    )
```

profile of v0, /device:TPU:81, one launch (start us, length us, event | category | flops | bytes accessed | tf_op | source)
XLA Modules:
  0.0 710.2 jit_solution(6092415604562765898)
XLA Ops:
  1.8 686.8 %while.19 = (s32[]{:T(128)}, bf16[1,256,384]{2,1,0:T(8,128)(2,1)S(1)}, bf16[1,256,384]{2,1,0:T(8,128)(2,1)S(1)}, f32[1,256,16]{1,2,0:T(8,128)S(1)}, f32[1,256,16...) while((s32[]{:T(128)}, ...), condition=%wide.region_9.10_spmd, body=%wide.region_0.9_spmd.sunk | while | flops 1021990656 | bytes 21182484 | solution.py:61
  16.2 4.6 collective-permute-start
  20.9 2.5 collective-permute-done
  37.8 4.4 collective-permute-start
  42.3 2.5 collective-permute-done
  59.3 4.4 collective-permute-start
  63.8 2.5 collective-permute-done
  80.8 4.4 collective-permute-start
  85.3 2.5 collective-permute-done
  102.2 4.4 collective-permute-start
  106.7 2.5 collective-permute-done
  123.7 4.4 collective-permute-start
  128.2 2.5 collective-permute-done
  145.1 4.4 collective-permute-start
  149.6 2.5 collective-permute-done
  166.6 4.4 collective-permute-start
  171.1 2.5 collective-permute-done
  188.0 4.4 collective-permute-start
  192.5 2.5 collective-permute-done
  209.5 4.4 collective-permute-start
  214.0 2.5 collective-permute-done
  230.9 4.4 collective-permute-start
  235.5 2.5 collective-permute-done
  252.4 4.4 collective-permute-start
  256.9 2.5 collective-permute-done
  273.9 4.4 collective-permute-start
  278.4 2.5 collective-permute-done
  295.3 4.4 collective-permute-start
  299.8 2.5 collective-permute-done
  316.8 4.4 collective-permute-start
  321.3 2.5 collective-permute-done
  338.2 4.4 collective-permute-start
  342.7 2.5 collective-permute-done
  359.7 4.4 collective-permute-start
  364.2 2.5 collective-permute-done
  381.1 4.4 collective-permute-start
  385.7 2.5 collective-permute-done
  402.6 4.4 collective-permute-start
  407.1 2.5 collective-permute-done
  424.1 4.4 collective-permute-start
  428.6 2.5 collective-permute-done
  445.5 4.4 collective-permute-start
  450.0 2.5 collective-permute-done
  467.0 4.4 collective-permute-start
  471.5 2.5 collective-permute-done
  488.4 4.4 collective-permute-start
  492.9 2.5 collective-permute-done
  509.9 4.4 collective-permute-start
  514.4 2.5 collective-permute-done
  531.3 4.4 collective-permute-start
  535.9 2.5 collective-permute-done
  552.8 4.4 collective-permute-start
  557.3 2.5 collective-permute-done
  574.3 4.4 collective-permute-start
  578.8 2.5 collective-permute-done
  595.7 4.4 collective-permute-start
  600.2 2.5 collective-permute-done
  617.2 4.4 collective-permute-start
  621.7 2.5 collective-permute-done
  638.6 4.4 collective-permute-start
  643.1 2.5 collective-permute-done
  660.1 4.4 collective-permute-start
  681.5 4.4 collective-permute-start
  688.6 21.5 %psum.7 = f32[1,256,16]{1,2,0:T(8,128)} all-reduce(f32[1,256,16]{1,2,0:T(8,128)S(1)} %broadcast_select_fusion.1), channel_id=1, replica_groups=mesh['data'=4,'stage'=8] {'stage'}, use_global_device_ids=true, to_apply=%region_10.11 | all-reduce | flops 4096 | bytes 32768 | tf_op jit(solution)/shard_map/psum | solution.py:63
  (1126 shorter events, 466.1 us)
Async XLA Ops:
  15.5 5.3 collective-permute-start.1
  16.2 7.2 %collective-permute-start = (bf16[1,256,384]{2,1,0:T(8,128)(2,1)S(1)}, bf16[1,256,384]{2,1,0:T(8,128)(2,1)S(1)}, u32[]{:S(2)}, u32[]{:S(2)}) collective-permute-start(bf16[1,256,384]{2,1,0:T(8,128)(2,1)S(1)} %get-tuple-element.419), channel_id=1, source_target_pairs={{0,1},{1,2},{2,3},{3,4},{4,5},{5,6},{6,7},{8,9},{9,10},{10,11},{11... | collective-permute-start | bytes 589832 | tf_op jit(solution)/shard_map/while/body/eval_jaxpr/ppermute | solution.py:55
  37.2 5.2 collective-permute-start.1
  37.8 7.0 collective-permute-start
  58.6 5.2 collective-permute-start.1
  59.3 7.0 collective-permute-start
  80.1 5.2 collective-permute-start.1
  80.8 7.0 collective-permute-start
  101.5 5.2 collective-permute-start.1
  102.2 7.0 collective-permute-start
  123.0 5.2 collective-permute-start.1
  123.7 7.0 collective-permute-start
  144.5 5.2 collective-permute-start.1
  145.1 7.0 collective-permute-start
  165.9 5.2 collective-permute-start.1
  166.6 7.0 collective-permute-start
  187.4 5.2 collective-permute-start.1
  188.0 7.0 collective-permute-start
  208.8 5.2 collective-permute-start.1
  209.5 7.0 collective-permute-start
  230.3 5.2 collective-permute-start.1
  230.9 7.0 collective-permute-start
  251.7 5.2 collective-permute-start.1
  252.4 7.0 collective-permute-start
  273.2 5.2 collective-permute-start.1
  273.9 7.0 collective-permute-start
  294.7 5.2 collective-permute-start.1
  295.3 7.0 collective-permute-start
  316.1 5.2 collective-permute-start.1
  316.8 7.0 collective-permute-start
  337.6 5.2 collective-permute-start.1
  338.2 7.0 collective-permute-start
  359.0 5.2 collective-permute-start.1
  359.7 7.0 collective-permute-start
  380.5 5.2 collective-permute-start.1
  381.1 7.0 collective-permute-start
  401.9 5.2 collective-permute-start.1
  402.6 7.0 collective-permute-start
  423.4 5.2 collective-permute-start.1
  424.1 7.0 collective-permute-start
  444.9 5.2 collective-permute-start.1
  445.5 7.0 collective-permute-start
  466.3 5.2 collective-permute-start.1
  467.0 7.0 collective-permute-start
  487.8 5.2 collective-permute-start.1
  488.4 7.0 collective-permute-start
  509.2 5.2 collective-permute-start.1
  509.9 7.0 collective-permute-start
  530.7 5.2 collective-permute-start.1
  531.3 7.0 collective-permute-start
  552.1 5.2 collective-permute-start.1
  552.8 7.0 collective-permute-start
  573.6 5.2 collective-permute-start.1
  574.3 7.0 collective-permute-start
  595.0 5.2 collective-permute-start.1
  595.7 7.0 collective-permute-start
  616.5 5.2 collective-permute-start.1
  617.2 7.0 collective-permute-start
  638.0 5.2 collective-permute-start.1
  638.6 7.0 collective-permute-start
  659.4 5.2 collective-permute-start.1
  660.1 7.0 collective-permute-start
  680.9 5.2 collective-permute-start.1
  681.5 7.0 collective-permute-start
  (160 other events, 465.3 us)
where the time goes:
time: 720 us; the launch traced here: 710 us
  matrix products  342 us (48%)
  starting transfers between devices  163 us (23%)
  waiting for transfers between devices  80.3 us (11%)
  local copies, waits for them, and re-layouts  51.8 us (7%)
  other arithmetic  45.8 us (6%)
  blocking collectives  21.5 us (3%)
    ppermute x32, starting transfers between devices, one_step(): sent_bound = lax.ppermute(hidden.astype(jnp.bfloat16), 'stage', fwd_pairs)  142 us
    ppermute x32, waiting for transfers between devices, one_step(): sent_bound = lax.ppermute(hidden.astype(jnp.bfloat16), 'stage', fwd_pairs)  80.2 us
    dot_general x32, matrix products, local_block(): jnp.einsum('bnf,fd->bnd', mlp_act, w_down_l, preferred_element_type=jnp.f...  79.3 us
    dot_general x32, matrix products, local_block(): jnp.einsum('bqhd,hde->bqe', attn_out, w_proj_l, preferred_element_type=jn...  68.6 us
    sub x32, matrix products, local_block(): attn_prob = jax.nn.softmax(scores, axis=-1).astype(jnp.bfloat16)  57.9 us
    dot_general x32, matrix products, local_block(): jnp.einsum('bnd,de->bne', normed, w_qkv_l, preferred_element_type=jnp.flo...  54.8 us
    dot_general x32, matrix products, one_step(): jnp.einsum('rnd,dc->rnc', normed, w_out, preferred_element_type=jnp.float32)  47.9 us
    dynamic_slice x64, local copies, waits for them, and re-layouts, one_step(): x_next = coef_keep[step_idx] * x_cur + coef_noise[step_idx] * noise_pred  39.8 us
  transfers between devices with their start and end apart: 64, of which 32 were waited for; matrix products, arithmetic and copies ran while one was open for 0% of the time, Pallas kernels for 0%

commit v1 on v0

v1 whole, which is shorter than its diff:
```python
import functools
import math

import jax
import jax.numpy as jnp
from jax import lax
from jax.experimental import pallas as pl
from jax.experimental.pallas import tpu as pltpu
from jax.sharding import PartitionSpec as P

LN_EPS = 1e-6
LOG2E = math.log2(math.e)
GELU_A = math.sqrt(2.0 / math.pi)
GELU_B = GELU_A * 0.044715


def normalize(hidden):
    scale = 1.0 / hidden.shape[0]
    mean = jnp.sum(hidden, axis=0, keepdims=True) * scale
    centered = hidden - mean
    var = jnp.sum(centered * centered, axis=0, keepdims=True) * scale
    return centered * lax.rsqrt(var + LN_EPS)


def dot(lhs, rhs):
    return jnp.dot(lhs, rhs, preferred_element_type=jnp.float32)


def kernel(stages, blocks, x_ref, w_in_ref, w_out_ref, qkv_hbm, proj_hbm, up_hbm, down_hbm, mod_ref, keep_ref, noise_ref, warm_hbm,
           out_ref, qkv_n, proj_n, up_n, down_n, warm_n, w_in_t, qkv_w, proj_w, up_w, down_w,
           recv, sent, x_recv, x_cur, h_scr, u_scr, qkv_scr, o_scr, act_scr,
           load_sem, recv_sem, send_sem, x_recv_sem, x_send_sem, last_send_sem, last_recv_sem):
    stage = lax.axis_index('stage')
    is_first = stage == 0
    is_last = stage == stages - 1
    steps = keep_ref.shape[0]
    width, tokens = h_scr.shape
    heads, head_dim = proj_hbm.shape[0], proj_hbm.shape[1]
    bf16 = jnp.bfloat16

    loads = [
        pltpu.make_async_copy(warm_hbm.at[:, jnp.maximum(stage - 1, 0), 0], warm_n, load_sem.at[0]),
        pltpu.make_async_copy(qkv_hbm, qkv_n, load_sem.at[1]),
        pltpu.make_async_copy(proj_hbm, proj_n, load_sem.at[2]),
        pltpu.make_async_copy(up_hbm, up_n, load_sem.at[3]),
        pltpu.make_async_copy(down_hbm, down_n, load_sem.at[4]),
    ]
    for copy in loads:
        copy.start()
    barrier = pltpu.get_barrier_semaphore()
    for ahead in range(1, stages):
        pl.semaphore_signal(barrier, inc=1, device_id={'stage': lax.rem(stage + ahead, stages)},
                            device_id_type=pl.DeviceIdType.MESH)

    w_in_t[...] = w_in_ref[...].T
    x_cur[...] = x_ref[...]
    for slot in range(2):
        x_recv[slot] = x_ref[...]
    loads[0].wait()
    for slot in range(2):
        recv[slot] = warm_n[slot].T
    loads[1].wait()
    qkv_w[...] = qkv_n[...].T
    loads[2].wait()
    proj_w[...] = proj_n[...].reshape(width, width).T
    loads[3].wait()
    up_w[...] = up_n[...].T
    loads[4].wait()
    down_w[...] = down_n[...].T
    pl.semaphore_wait(barrier, stages - 1)

    next_id = {'stage': lax.rem(stage + 1, stages)}

    def hidden_copy(step):
        return pltpu.make_async_remote_copy(
            src_ref=sent.at[step], dst_ref=recv.at[step + 2], send_sem=send_sem.at[step], recv_sem=recv_sem.at[step + 2],
            device_id=next_id, device_id_type=pl.DeviceIdType.MESH)

    def latent_copy(step):
        return pltpu.make_async_remote_copy(
            src_ref=x_recv.at[step + 2], dst_ref=x_recv.at[step + 2], send_sem=x_send_sem.at[step], recv_sem=x_recv_sem.at[step + 2],
            device_id=next_id, device_id_type=pl.DeviceIdType.MESH)

    first_trips = steps - 2 * (stages - 1)
    trips = first_trips + 2 * stage

    def one_step(step, carry):
        @pl.when(is_first)
        def _():
            @pl.when(step >= 2)
            def _():
                latent_copy(step - 2).wait_recv()
            h_scr[...] = dot(w_in_t[...], x_recv[step].astype(bf16))

        @pl.when(jnp.logical_not(is_first))
        def _():
            @pl.when(step >= 2)
            def _():
                hidden_copy(step - 2).wait_recv()
            h_scr[...] = recv[step].astype(jnp.float32)

        mod_t = mod_ref[step].T
        parts = width // 128

        def mod_col(row, plus=0.0):
            cols = [mod_t[:, row * parts + part:row * parts + part + 1] for part in range(parts)]
            col = jnp.concatenate(cols, axis=0) + plus
            return jnp.broadcast_to(col, (width, tokens))

        hidden = h_scr[...]
        u_scr[...] = (normalize(hidden) * mod_col(1, 1.0) + mod_col(0)).astype(bf16)
        qkv_scr[...] = dot(qkv_w[...], u_scr[...]).astype(bf16)
        factor = LOG2E * head_dim ** -0.5
        for head in range(heads):
            lo = head * head_dim
            query = qkv_scr[lo:lo + head_dim]
            key = qkv_scr[width + lo:width + lo + head_dim]
            value = qkv_scr[2 * width + lo:2 * width + lo + head_dim]
            scores = dot(key.T, query)
            top = jnp.max(scores, axis=0, keepdims=True)
            expo = jnp.exp2((scores - top) * factor)
            total = jnp.sum(expo, axis=0, keepdims=True)
            o_scr[lo:lo + head_dim] = (dot(value, expo.astype(bf16)) * (1.0 / total)).astype(bf16)
        hidden = h_scr[...] + mod_col(2) * dot(proj_w[...], o_scr[...])
        h_scr[...] = hidden
        u_scr[...] = (normalize(hidden) * mod_col(4, 1.0) + mod_col(3)).astype(bf16)
        chunk = width
        for lo in range(0, 4 * width, chunk):
            pre = dot(up_w[lo:lo + chunk], u_scr[...])
            half = 0.5 * pre
            act_scr[lo:lo + chunk] = (half * jnp.tanh(pre * (GELU_A + GELU_B * (pre * pre))) + half).astype(bf16)
        hidden = h_scr[...] + mod_col(5) * dot(down_w[...], act_scr[...])

        @pl.when(jnp.logical_not(is_last))
        def _():
            sent[step] = hidden.astype(bf16)
            hidden_copy(step).start()

        @pl.when(is_last)
        def _():
            noise = dot(w_out_ref[...], normalize(hidden).astype(bf16))
            x_next = keep_ref[step] * x_cur[...] + noise_ref[step] * noise
            x_cur[...] = x_next

            @pl.when(step + 2 < first_trips)
            def _():
                x_recv[step + 2] = x_next
                latent_copy(step).start()
        return carry

    lax.fori_loop(0, trips, one_step, 0)

    def final_copy(ahead):
        return pltpu.make_async_remote_copy(
            src_ref=x_cur, dst_ref=out_ref, send_sem=last_send_sem.at[ahead], recv_sem=last_recv_sem,
            device_id={'stage': lax.rem(stage + ahead, stages)}, device_id_type=pl.DeviceIdType.MESH)

    @pl.when(is_last)
    def _():
        for ahead in range(1, stages):
            final_copy(ahead).start()
        out_ref[...] = x_cur[...]
        for ahead in range(1, stages):
            final_copy(ahead).wait_send()

        def drain(step, carry):
            latent_copy(step).wait_send()
            return carry
        lax.fori_loop(0, first_trips - 2, drain, 0)

    @pl.when(jnp.logical_not(is_last))
    def _():
        def drain(step, carry):
            hidden_copy(step).wait_send()
            return carry
        lax.fori_loop(0, trips, drain, 0)
        final_copy(1).wait_recv()


def solution(mesh):
    stages = mesh.shape['stage']

    def shard_body(x_init, w_in, w_out, w_qkv, w_proj, w_up, w_down, mod_table, coef_keep, coef_noise, h_warm):
        steps = coef_keep.shape[0]
        rows, tokens, chan = x_init.shape
        blocks, width = w_qkv.shape[0], w_qkv.shape[1]
        mlp = w_up.shape[2]
        heads, head_dim = w_proj.shape[1], w_proj.shape[2]
        bf16, f32 = jnp.bfloat16, jnp.float32
        vmem = pl.BlockSpec(memory_space=pltpu.VMEM)
        smem = pl.BlockSpec(memory_space=pltpu.SMEM)
        hbm = pl.BlockSpec(memory_space=pl.ANY)
        mod = mod_table.reshape(steps, 6 * width // 128, 128)
        mod = jnp.pad(mod, ((0, 0), (0, -mod.shape[1] % 8), (0, 0)))
        out = pl.pallas_call(
            functools.partial(kernel, stages, blocks),
            out_shape=jax.ShapeDtypeStruct((chan, tokens), f32),
            in_specs=[vmem, vmem, vmem, hbm, hbm, hbm, hbm, vmem, smem, smem, hbm],
            out_specs=vmem,
            scratch_shapes=[
                pltpu.VMEM((width, 3 * width), bf16),
                pltpu.VMEM((heads, head_dim, width), bf16),
                pltpu.VMEM((width, mlp), bf16),
                pltpu.VMEM((mlp, width), bf16),
                pltpu.VMEM((2, tokens, width), bf16),
                pltpu.VMEM((width, chan), bf16),
                pltpu.VMEM((3 * width, width), bf16),
                pltpu.VMEM((width, width), bf16),
                pltpu.VMEM((mlp, width), bf16),
                pltpu.VMEM((width, mlp), bf16),
                pltpu.VMEM((steps, width, tokens), bf16),
                pltpu.VMEM((steps, width, tokens), bf16),
                pltpu.VMEM((steps, chan, tokens), f32),
                pltpu.VMEM((chan, tokens), f32),
                pltpu.VMEM((width, tokens), f32),
                pltpu.VMEM((width, tokens), bf16),
                pltpu.VMEM((3 * width, tokens), bf16),
                pltpu.VMEM((width, tokens), bf16),
                pltpu.VMEM((mlp, tokens), bf16),
                pltpu.SemaphoreType.DMA((5,)),
                pltpu.SemaphoreType.DMA((steps,)),
                pltpu.SemaphoreType.DMA((steps,)),
                pltpu.SemaphoreType.DMA((steps,)),
                pltpu.SemaphoreType.DMA((steps,)),
                pltpu.SemaphoreType.DMA((stages,)),
                pltpu.SemaphoreType.DMA,
            ],
            compiler_params=pltpu.CompilerParams(collective_id=0, has_side_effects=True, vmem_limit_bytes=56 * 1024 * 1024),
            name='stage_loop',
        )(jnp.swapaxes(x_init, 1, 2)[0], w_in, jnp.swapaxes(w_out, 0, 1), w_qkv[0], w_proj[0], w_up[0], w_down[0], mod,
          coef_keep, coef_noise, h_warm)
        return jnp.swapaxes(out, 0, 1)[None]

    return jax.shard_map(
        shard_body,
        mesh=mesh,
        in_specs=(P('data'), P(), P(), P('stage'), P('stage'), P('stage'), P('stage'), P(None, 'stage'), P(), P(), P(None, None, 'data')),
        out_specs=P('data'),
        check_vma=False,
    )
```

time: 720 us -> 155 us (0.22); the launches traced: 710 us -> 154 us
  matrix products: 342 us -> 0 us
  starting transfers between devices: 163 us -> 0 us
  Pallas kernels: 0 us -> 151 us
  waiting for transfers between devices: 80.3 us -> 0 us
  local copies, waits for them, and re-layouts: 51.8 us -> 2.14 us
  other arithmetic: 45.8 us -> 1.67 us
  blocking collectives: 21.5 us -> 0 us
    dot_general x160 -> x0, matrix products: 284 us -> none  [the longest x32 79.3 us: local_block(): jnp.einsum('bnf,fd->bnd', mlp_act, w_down_l, preferred_element_type=jnp.f...]
    ppermute x64 -> x0, starting transfers between devices: 163 us -> none  [the longest x32 142 us: one_step(): sent_bound = lax.ppermute(hidden.astype(jnp.bfloat16), 'stage', fwd_pairs)]
    pallas_call x0 -> x1, Pallas kernels: none -> 151 us  [shard_body(): pl.pallas_call(functools.partial(kernel, stages, blocks), out_shape=jax.S...]
    ppermute x64 -> x0, waiting for transfers between devices: 80.3 us -> none  [the longest x32 80.2 us: one_step(): sent_bound = lax.ppermute(hidden.astype(jnp.bfloat16), 'stage', fwd_pairs)]
    sub x32 -> x0, matrix products: 57.9 us -> none  [local_block(): attn_prob = jax.nn.softmax(scores, axis=-1).astype(jnp.bfloat16)]
    dynamic_slice x64 -> x0, local copies, waits for them, and re-layouts: 39.8 us -> none  [one_step(): x_next = coef_keep[step_idx] * x_cur + coef_noise[step_idx] * noise_pred]
    slice x32 -> x0, other arithmetic: 25.9 us -> none  [local_block(): mod_l[5]]
    psum x1 -> x0, blocking collectives: 21.5 us -> none  [shard_body(): return lax.psum(x_last, 'stage')]
  transfers between devices with their start and end apart: 64 -> 0, of which waited for: 32 -> 0; matrix products, arithmetic and copies ran while one was open for 0% -> 0% of each run, Pallas kernels for 0% -> 0%
where the time goes in v1:
time: 155 us; the launch traced here: 154 us
  Pallas kernels  151 us (97%)
  local copies, waits for them, and re-layouts  2.14 us (1%)
  other arithmetic  1.67 us (1%)
    pallas_call x1, Pallas kernels, shard_body(): pl.pallas_call(functools.partial(kernel, stages, blocks), out_shape=jax.S...  151 us

profile of v1, /device:TPU:81, one launch (start us, length us, event | category | flops | bytes accessed | tf_op | source)
XLA Modules:
  0.0 154.4 jit_solution(7407753609634246779)
XLA Ops:
  0.0 1.7 %reduce = f32[32,6,384]{2,1,0:T(8,128)S(1)} reduce(f32[32,1,6,384]{3,1,2,0:T(1,128)} %param.18, f32[]{:T(128)} %constant.12), dimensions={1}, to_apply=%param.18.reduce_sub_computation | reduce | bytes 589828 | tf_op args[7]
  1.7 0.8 pad.4.mod_ref
  2.5 150.6 %stage_loop.1 = f32[16,256]{1,0:T(8,128)} custom-call(f32[16,256]{1,0:T(8,128)} %bitcast.16, bf16[16,384]{1,0:T(8,128)(2,1)} %w_in_ref.1, bf16[16,384]{1,0:T(8,128)(2,1)} %bitcast.17, bf16[384,1152]{1,0:T(8,128)(2,1)} %bitcast.13, bf16[6,64,384]{2,1,0:T(8,128)(2,1)} %bitcast.14, bf16[384,1536]{1,0:T(8,128)(2,1)} %bitcast.11, bf16[1536,384]{1,0:T(8,128)(2,1)} %bitcast.12, ...), custom_call_target="tpu_custom_call" | custom-call | tf_op jit(solution)/shard_map/stage_loop/pallas_call | solution.py:195
  153.1 1.3 copy.13
  (1 shorter events, 0.0 us)

commit v2 on v1

v2 whole, which is shorter than its diff:
```python
import functools
import math

import jax
import jax.numpy as jnp
from jax import lax
from jax.experimental import pallas as pl
from jax.experimental.pallas import tpu as pltpu
from jax.sharding import PartitionSpec as P

LN_EPS = 1e-6
LOG2E = math.log2(math.e)
GELU_A = math.sqrt(2.0 / math.pi)
GELU_B = GELU_A * 0.044715
CHUNK = 256
MESH = pl.DeviceIdType.MESH


def fold(rows):
    while rows.shape[0] % 16 == 0:
        half = rows.shape[0] // 2
        rows = rows[:half] + rows[half:]
    parts = [rows[lo:lo + 8] for lo in range(0, rows.shape[0], 8)]
    while len(parts) > 1:
        parts = [a + b for a, b in zip(parts[::2], parts[1::2])] + parts[len(parts) - len(parts) % 2:]
    return jnp.sum(parts[0], axis=0, keepdims=True)


def normalize(hidden):
    scale = 1.0 / hidden.shape[0]
    centered = hidden - fold(hidden) * scale
    var = fold(centered * centered) * scale
    return centered * lax.rsqrt(var + LN_EPS)


def dot(lhs, rhs):
    return jnp.dot(lhs, rhs, preferred_element_type=jnp.float32)


def kernel(stages, x_ref, w_in_ref, w_out_ref, qkv_hbm, proj_hbm, up_hbm, down_hbm, mod_ref, keep_ref, noise_ref, warm_hbm,
           out_ref, qkv_n, proj_n, up_n, down_n, warm_n, w_in_t, qkv_w, proj_w, up_w, down_w, mod_s, select, lanes,
           recv, sent, x_recv, x_cur, h_last, h_scr, u_scr, o_scr, load_sem, recv_sem, send_sem, x_recv_sem, x_send_sem, last_send_sem, last_recv_sem):
    stage = lax.axis_index('stage')
    is_first = stage == 0
    is_last = stage == stages - 1
    steps = keep_ref.shape[0]
    width, tokens = h_last.shape
    heads, head_dim = proj_hbm.shape[0], proj_hbm.shape[1]
    mlp = up_w.shape[0]
    lanes_k = select.shape[1]
    bf16, f32 = jnp.bfloat16, jnp.float32

    loads = [
        pltpu.make_async_copy(warm_hbm.at[:, jnp.maximum(stage - 1, 0), 0], warm_n, load_sem.at[0]),
        pltpu.make_async_copy(qkv_hbm, qkv_n, load_sem.at[1]),
        pltpu.make_async_copy(proj_hbm, proj_n, load_sem.at[2]),
        pltpu.make_async_copy(up_hbm, up_n, load_sem.at[3]),
        pltpu.make_async_copy(down_hbm, down_n, load_sem.at[4]),
    ]
    for copy in loads:
        copy.start()
    barrier = pltpu.get_barrier_semaphore()
    for ahead in range(1, stages):
        pl.semaphore_signal(barrier, inc=1, device_id={'stage': lax.rem(stage + ahead, stages)}, device_id_type=MESH)

    mod_rows = mod_ref.shape[0] // steps
    parts = width // 128
    pad = lanes_k // 3
    row_id = lax.broadcasted_iota(jnp.int32, (mod_rows, 128), 0) // parts
    plus = jnp.where((row_id == 1) | (row_id == 4), 1.0, 0.0)
    limit = float(jnp.finfo(bf16).max)
    gap = jnp.zeros((pad - mod_rows, 128), f32)

    def split_mod(step, carry):
        rows = mod_ref[pl.ds(step * mod_rows, mod_rows)] + plus
        high = jnp.clip(rows, -limit, limit).astype(bf16).astype(f32)
        rest = rows - high
        mid = rest.astype(bf16).astype(f32)
        terms = jnp.concatenate([high, gap, mid, gap, rest - mid, gap], axis=0)
        mod_s[step] = terms.T.astype(bf16)
        return carry

    lax.fori_loop(0, steps, split_mod, 0)
    term = lax.broadcasted_iota(jnp.int32, (lanes_k, 256), 0) % pad
    column = lax.broadcasted_iota(jnp.int32, (lanes_k, 256), 1) // 128
    for pair in range(3):
        for part in range(parts):
            pick = term == (2 * pair + column) * parts + part
            select[pair * parts + part] = jnp.where(pick, 1.0, 0.0).astype(bf16)

    def fill_lanes(step, pair, part):
        both = dot(mod_s[step], select[pair * parts + part])
        for side in range(2):
            lanes[2 * pair + side, part * 128:part * 128 + 128] = both[:, side * 128:side * 128 + 128]

    halves = [slice(lo, lo + 128) for lo in range(0, tokens, 128)]

    w_in_t[...] = w_in_ref[...].T
    x_cur[...] = x_ref[...]
    for slot in range(2):
        x_recv[slot] = x_ref[...]
    loads[0].wait()
    for slot in range(2):
        recv[slot] = warm_n[slot].T
    loads[1].wait()
    qkv_w[...] = qkv_n[...].T
    loads[2].wait()
    proj_w[...] = proj_n[...].reshape(width, width).T
    loads[3].wait()
    up_w[...] = up_n[...].T * jnp.asarray(0.5, bf16)
    loads[4].wait()
    down_w[...] = down_n[...].T
    pl.semaphore_wait(barrier, stages - 1)

    next_id = {'stage': lax.rem(stage + 1, stages)}

    def hidden_copy(step):
        return pltpu.make_async_remote_copy(
            src_ref=sent.at[step], dst_ref=recv.at[step + 2], send_sem=send_sem.at[step], recv_sem=recv_sem.at[step + 2],
            device_id=next_id, device_id_type=MESH)

    def latent_copy(step):
        return pltpu.make_async_remote_copy(
            src_ref=x_recv.at[step + 2], dst_ref=x_recv.at[step + 2], send_sem=x_send_sem.at[step], recv_sem=x_recv_sem.at[step + 2],
            device_id=next_id, device_id_type=MESH)

    first_trips = steps - 2 * (stages - 1)
    trips = first_trips + 2 * stage

    def norm_into(hidden, scale_row, shift_row, half):
        u_scr[:, half] = (normalize(hidden) * lanes[scale_row] + lanes[shift_row]).astype(bf16)

    def block(step, hidden_in, beside=lambda: None):
        for part in range(parts):
            fill_lanes(step, 0, part)
        for half in halves:
            norm_into(hidden_in(half), 1, 0, half)
        normed = u_scr[...]
        key = dot(qkv_w[width:2 * width], normed).astype(bf16)
        query = dot(qkv_w[:width], normed).astype(bf16)
        factor = LOG2E * head_dim ** -0.5

        def head(rows, index):
            return rows[index * head_dim:(index + 1) * head_dim]

        def score(index):
            return dot(head(key, index).T, head(query, index))

        def softmax(scores):
            top = jnp.max(scores, axis=0, keepdims=True)
            expo = jnp.exp2((scores - top) * factor)
            return expo.astype(bf16), 1.0 / fold(expo)

        scores = {0: score(0), 1: score(1)}
        value = dot(qkv_w[2 * width:], normed).astype(bf16)
        fills = [(pair, part) for pair in (1, 2) for part in range(parts)]
        split = 256 // head_dim
        proj = [None, None]
        mid = width // 2

        def project(lo, hi):
            rows = o_scr[lo:hi]
            for side in range(2):
                piece = dot(proj_w[side * mid:side * mid + mid, lo:hi], rows)
                proj[side] = piece if proj[side] is None else proj[side] + piece

        for index in range(heads):
            if index + 2 < heads:
                scores[index + 2] = score(index + 2)
            cur = scores.pop(index)
            done = [softmax(cur[:, half]) for half in halves]
            expo = jnp.concatenate([pair[0] for pair in done], axis=1)
            inverse = jnp.concatenate([pair[1] for pair in done], axis=1)
            o_scr[index * head_dim:(index + 1) * head_dim] = (dot(head(value, index), expo) * inverse).astype(bf16)
            if index < len(fills):
                fill_lanes(step, *fills[index])
            if index == 0:
                beside()
            if index == split - 1:
                project(0, 256)
        project(256, width)
        for half in halves:
            hidden = hidden_in(half) + lanes[2] * jnp.concatenate([side[:, half] for side in proj], axis=0)
            h_scr[:, half] = hidden
            norm_into(hidden, 4, 3, half)
        normed = u_scr[...]
        count = mlp // CHUNK
        ups = {}

        def up(index):
            return dot(up_w[index * CHUNK:(index + 1) * CHUNK], normed)

        ups[0] = up(0)
        total = [None, None]
        for index in range(count):
            if index + 1 < count:
                ups[index + 1] = up(index + 1)
            pre = ups.pop(index)
            act = (pre * jnp.tanh(pre * (2.0 * GELU_A + 8.0 * GELU_B * (pre * pre))) + pre).astype(bf16)
            for side in range(2):
                piece = dot(down_w[side * mid:side * mid + mid, index * CHUNK:(index + 1) * CHUNK], act)
                total[side] = piece if total[side] is None else total[side] + piece
        for half in halves:
            yield half, h_scr[:, half] + lanes[5] * jnp.concatenate([side[:, half] for side in total], axis=0)

    def send(step, columns):
        for half, hidden in columns:
            sent[step, :, half] = hidden.astype(bf16)
        hidden_copy(step).start()

    def received(step):
        return lambda half: recv[step, :, half].astype(f32)

    def wait_hidden(step):
        @pl.when(step >= 2)
        def _():
            hidden_copy(step - 2).wait_recv()

    def first_step(step, carry):
        @pl.when(step >= 2)
        def _():
            latent_copy(step - 2).wait_recv()
        embedded = dot(w_in_t[...], x_recv[step].astype(bf16))
        h_last[...] = embedded
        send(step, block(step, lambda half: h_last[:, half]))
        return carry

    def middle_step(step, carry):
        wait_hidden(step)
        send(step, block(step, received(step)))
        return carry

    def advance(step):
        normed = jnp.concatenate([normalize(h_last[:, half]).astype(bf16) for half in halves], axis=1)
        noise = dot(w_out_ref[...], normed)
        x_next = keep_ref[step] * x_cur[...] + noise_ref[step] * noise
        x_cur[...] = x_next
        return x_next

    def last_step(step, carry):
        wait_hidden(step)
        before = jnp.maximum(step - 1, 0)

        def beside():
            x_next = jnp.where(step > 0, advance(before), x_ref[...])
            x_cur[...] = x_next
            x_recv[jnp.minimum(before + 2, steps - 1)] = x_next

        for half, hidden in block(step, received(step), beside):
            h_last[:, half] = hidden

        @pl.when((step > 0) & (before + 2 < first_trips))
        def _():
            latent_copy(before).start()
        return carry

    def final_copy(ahead):
        return pltpu.make_async_remote_copy(
            src_ref=x_cur, dst_ref=out_ref, send_sem=last_send_sem.at[ahead], recv_sem=last_recv_sem,
            device_id={'stage': lax.rem(stage + ahead, stages)}, device_id_type=MESH)

    @pl.when(is_first)
    def _():
        lax.fori_loop(0, first_trips, first_step, 0)

    @pl.when(jnp.logical_not(is_first | is_last))
    def _():
        lax.fori_loop(0, trips, middle_step, 0)

    @pl.when(is_last)
    def _():
        h_last[...] = jnp.zeros_like(h_last)
        lax.fori_loop(0, steps, last_step, 0)
        out_ref[...] = advance(steps - 1)
        for ahead in range(1, stages):
            final_copy(ahead).start()
        for ahead in range(1, stages):
            final_copy(ahead).wait_send()

        def drain(step, carry):
            latent_copy(step).wait_send()
            return carry
        lax.fori_loop(0, first_trips - 2, drain, 0)

    @pl.when(jnp.logical_not(is_last))
    def _():
        def drain(step, carry):
            hidden_copy(step).wait_send()
            return carry
        lax.fori_loop(0, trips, drain, 0)
        final_copy(1).wait_recv()


def solution(mesh):
    stages = mesh.shape['stage']

    def shard_body(x_init, w_in, w_out, w_qkv, w_proj, w_up, w_down, mod_table, coef_keep, coef_noise, h_warm):
        steps = coef_keep.shape[0]
        tokens, chan = x_init.shape[1], x_init.shape[2]
        width, mlp = w_up.shape[1], w_up.shape[2]
        heads, head_dim = w_proj.shape[1], w_proj.shape[2]
        mod_rows = mod_table.shape[2] * width // 128
        lanes_k = 3 * (mod_rows + -mod_rows % 8)
        bf16, f32 = jnp.bfloat16, jnp.float32
        vmem = pl.BlockSpec(memory_space=pltpu.VMEM)
        smem = pl.BlockSpec(memory_space=pltpu.SMEM)
        hbm = pl.BlockSpec(memory_space=pl.ANY)
        out = pl.pallas_call(
            functools.partial(kernel, stages),
            out_shape=jax.ShapeDtypeStruct((chan, tokens), f32),
            in_specs=[vmem, vmem, vmem, hbm, hbm, hbm, hbm, vmem, smem, smem, hbm],
            out_specs=vmem,
            scratch_shapes=[
                pltpu.VMEM((width, 3 * width), bf16),
                pltpu.VMEM((heads, head_dim, width), bf16),
                pltpu.VMEM((width, mlp), bf16),
                pltpu.VMEM((mlp, width), bf16),
                pltpu.VMEM((2, tokens, width), bf16),
                pltpu.VMEM((width, chan), bf16),
                pltpu.VMEM((3 * width, width), bf16),
                pltpu.VMEM((width, width), bf16),
                pltpu.VMEM((mlp, width), bf16),
                pltpu.VMEM((width, mlp), bf16),
                pltpu.VMEM((steps, 128, lanes_k), bf16),
                pltpu.VMEM((3 * width // 128, lanes_k, 256), bf16),
                pltpu.VMEM((6, width, 128), f32),
                pltpu.VMEM((steps, width, tokens), bf16),
                pltpu.VMEM((steps, width, tokens), bf16),
                pltpu.VMEM((steps, chan, tokens), f32),
                pltpu.VMEM((chan, tokens), f32),
                pltpu.VMEM((width, tokens), f32),
                pltpu.VMEM((width, tokens), f32),
                pltpu.VMEM((width, tokens), bf16),
                pltpu.VMEM((width, tokens), bf16),
                pltpu.SemaphoreType.DMA((5,)),
                pltpu.SemaphoreType.DMA((steps,)),
                pltpu.SemaphoreType.DMA((steps,)),
                pltpu.SemaphoreType.DMA((steps,)),
                pltpu.SemaphoreType.DMA((steps,)),
                pltpu.SemaphoreType.DMA((stages,)),
                pltpu.SemaphoreType.DMA,
            ],
            compiler_params=pltpu.CompilerParams(collective_id=0, has_side_effects=True, vmem_limit_bytes=56 * 1024 * 1024),
            name='stage_loop',
        )(jnp.swapaxes(x_init, 1, 2)[0], w_in, jnp.swapaxes(w_out, 0, 1), w_qkv[0], w_proj[0], w_up[0], w_down[0],
          mod_table.reshape(steps * mod_rows, 128), coef_keep, coef_noise, h_warm)
        return jnp.swapaxes(out, 0, 1)[None]

    return jax.shard_map(
        shard_body,
        mesh=mesh,
        in_specs=(P('data'), P(), P(), P('stage'), P('stage'), P('stage'), P('stage'), P(None, 'stage'), P(), P(), P(None, None, 'data')),
        out_specs=P('data'),
        check_vma=False,
    )
```

time: 155 us -> 112 us (0.72)
  Pallas kernels: 151 us -> 110 us
  other arithmetic: 1.67 us -> 0 us
    pallas_call x1, Pallas kernels: 151 us -> 110 us  [shard_body(): pl.pallas_call(functools.partial(kernel, stages), out_shape=jax.ShapeDtyp...]
    unnamed x1 -> x0, other arithmetic: 1.67 us -> none
where the time goes in v2:
time: 112 us; the launch traced here: 111 us
  Pallas kernels  110 us (98%)
  local copies, waits for them, and re-layouts  1.32 us (1%)
    pallas_call x1, Pallas kernels, shard_body(): pl.pallas_call(functools.partial(kernel, stages), out_shape=jax.ShapeDtyp...  110 us

profile of v2, /device:TPU:81, one launch (start us, length us, event | category | flops | bytes accessed | tf_op | source)
XLA Modules:
  0.0 111.4 jit_solution(10150318981020749448)
XLA Ops:
  0.0 110.1 %stage_loop.1 = f32[16,256]{1,0:T(8,128)} custom-call(f32[16,256]{1,0:T(8,128)} %bitcast.18, bf16[16,384]{1,0:T(8,128)(2,1)} %w_in_ref.1, bf16[16,384]{1,0:T(8,128)(2,1)} %bitcast.19, bf16[384,1152]{1,0:T(8,128)(2,1)} %bitcast.14, bf16[6,64,384]{2,1,0:T(8,128)(2,1)} %bitcast.15, bf16[384,1536]{1,0:T(8,128)(2,1)} %bitcast.12, bf16[1536,384]{1,0:T(8,128)(2,1)} %bitcast.13, ...), custom_call_target="tpu_custom_call" | custom-call | tf_op jit(solution)/shard_map/stage_loop/pallas_call | solution.py:308
  110.1 1.3 %copy.13 = f32[1,256,16]{1,2,0:T(8,128)} copy(f32[1,256,16]{1,2,0:T(8,128)} %bitcast.17) | data formatting | bytes 32768

commit v3 on v2

--- a/solution.py
+++ b/solution.py
@@ -12,7 +12,7 @@
 LOG2E = math.log2(math.e)
 GELU_A = math.sqrt(2.0 / math.pi)
 GELU_B = GELU_A * 0.044715
-CHUNK = 256
+UNIT = 64
 MESH = pl.DeviceIdType.MESH
 
 
@@ -47,7 +47,6 @@
     width, tokens = h_last.shape
     heads, head_dim = proj_hbm.shape[0], proj_hbm.shape[1]
     mlp = up_w.shape[0]
-    lanes_k = select.shape[1]
     bf16, f32 = jnp.bfloat16, jnp.float32
 
     loads = [
@@ -65,31 +64,35 @@
 
     mod_rows = mod_ref.shape[0] // steps
     parts = width // 128
-    pad = lanes_k // 3
+    pad = mod_rows + -mod_rows % 8
     row_id = lax.broadcasted_iota(jnp.int32, (mod_rows, 128), 0) // parts
     plus = jnp.where((row_id == 1) | (row_id == 4), 1.0, 0.0)
     limit = float(jnp.finfo(bf16).max)
     gap = jnp.zeros((pad - mod_rows, 128), f32)
+    rest_rows = jnp.zeros((128 - 3 * pad, 128), f32)
 
     def split_mod(step, carry):
         rows = mod_ref[pl.ds(step * mod_rows, mod_rows)] + plus
         high = jnp.clip(rows, -limit, limit).astype(bf16).astype(f32)
         rest = rows - high
         mid = rest.astype(bf16).astype(f32)
-        terms = jnp.concatenate([high, gap, mid, gap, rest - mid, gap], axis=0)
+        terms = jnp.concatenate([high, gap, mid, gap, rest - mid, gap, rest_rows], axis=0)
         mod_s[step] = terms.T.astype(bf16)
         return carry
 
     lax.fori_loop(0, steps, split_mod, 0)
-    term = lax.broadcasted_iota(jnp.int32, (lanes_k, 256), 0) % pad
-    column = lax.broadcasted_iota(jnp.int32, (lanes_k, 256), 1) // 128
+    term = lax.broadcasted_iota(jnp.int32, (128, 256), 0)
+    term = jnp.where(term < 3 * pad, term % pad, -1)
+    column = lax.broadcasted_iota(jnp.int32, (128, 256), 1) // 128
     for pair in range(3):
         for part in range(parts):
             pick = term == (2 * pair + column) * parts + part
             select[pair * parts + part] = jnp.where(pick, 1.0, 0.0).astype(bf16)
 
-    def fill_lanes(step, pair, part):
-        both = dot(mod_s[step], select[pair * parts + part])
+    def fill(step, pair, part):
+        return dot(mod_s[step], select[pair * parts + part])
+
+    def store_fill(pair, part, both):
         for side in range(2):
             lanes[2 * pair + side, part * 128:part * 128 + 128] = both[:, side * 128:side * 128 + 128]
 
@@ -110,6 +113,8 @@
     up_w[...] = up_n[...].T * jnp.asarray(0.5, bf16)
     loads[4].wait()
     down_w[...] = down_n[...].T
+    for part in range(parts):
+        store_fill(0, part, fill(0, 0, part))
     pl.semaphore_wait(barrier, stages - 1)
 
     next_id = {'stage': lax.rem(stage + 1, stages)}
@@ -127,89 +132,176 @@
     first_trips = steps - 2 * (stages - 1)
     trips = first_trips + 2 * stage
 
-    def norm_into(hidden, scale_row, shift_row, half):
-        u_scr[:, half] = (normalize(hidden) * lanes[scale_row] + lanes[shift_row]).astype(bf16)
+    row_units = [slice(lo, lo + UNIT) for lo in range(0, width, UNIT)]
+
+    def to_tile(rows):
+        while rows.shape[0] > 8:
+            mid = rows.shape[0] // 2
+            rows = rows[:mid] + rows[mid:]
+        return rows
+
+    def mean_of(tiles_of_half):
+        total = tiles_of_half[0::2]
+        total = [a + b for a, b in zip(total, tiles_of_half[1::2])]
+        while len(total) > 1:
+            total = [a + b for a, b in zip(total[::2], total[1::2])] + total[len(total) - len(total) % 2:]
+        return jnp.sum(total[0], axis=0, keepdims=True) * (1.0 / width)
+
+    def norm_store(sums, scale_row, shift_row):
+        stats = []
+        for half, tiles_of_half in zip(halves, sums):
+            mean = mean_of(tiles_of_half)
+            squares = []
+            for rows in row_units:
+                centered = h_scr[rows, half] - mean
+                squares.append(to_tile(centered * centered))
+            stats.append((mean, lax.rsqrt(mean_of(squares) + LN_EPS)))
+        for rows in row_units:
+            for half, (mean, rstd) in zip(halves, stats):
+                u_scr[rows, half] = ((h_scr[rows, half] - mean) * rstd * lanes[scale_row, rows] + lanes[shift_row, rows]).astype(bf16)
+
+    quarter = width // 2
+    each = quarter // UNIT
+
+    row_units = [slice(lo, lo + UNIT) for lo in range(0, width, UNIT)]
+
+    def to_tile(rows):
+        while rows.shape[0] > 8:
+            mid = rows.shape[0] // 2
+            rows = rows[:mid] + rows[mid:]
+        return rows
+
+    def mean_of(tiles_of_half):
+        total = tiles_of_half[0::2]
+        total = [a + b for a, b in zip(total, tiles_of_half[1::2])]
+        while len(total) > 1:
+            total = [a + b for a, b in zip(total[::2], total[1::2])] + total[len(total) - len(total) % 2:]
+        return jnp.sum(total[0], axis=0, keepdims=True) * (1.0 / width)
+
+    def norm_store(sums, scale_row, shift_row):
+        stats = []
+        for half, tiles_of_half in zip(halves, sums):
+            mean = mean_of(tiles_of_half)
+            squares = []
+            for rows in row_units:
+                centered = h_scr[rows, half] - mean
+                squares.append(to_tile(centered * centered))
+            stats.append((mean, lax.rsqrt(mean_of(squares) + LN_EPS)))
+        for rows in row_units:
+            for half, (mean, rstd) in zip(halves, stats):
+                u_scr[rows, half] = ((h_scr[rows, half] - mean) * rstd * lanes[scale_row, rows] + lanes[shift_row, rows]).astype(bf16)
+
+    quarter = width // 2
+    each = quarter // UNIT
+
+    def tiles(rows):
+        return rows[:256], jnp.concatenate([zeros_half, rows[256:]], axis=0)
+
+    def weight(ref, row, register):
+        lo = 0 if register == 0 else width - 256
+        return ref[row:row + UNIT, lo:lo + 256]
 
     def block(step, hidden_in, beside=lambda: None):
-        for part in range(parts):
-            fill_lanes(step, 0, part)
-        for half in halves:
-            norm_into(hidden_in(half), 1, 0, half)
+        fills = {(pair, part): fill(step, pair, part) for pair in (1, 2) for part in range(parts)}
+        sums = [[], []]
+        for rows in row_units:
+            for side, half in enumerate(halves):
+                hidden = hidden_in(half, rows)
+                h_scr[rows, half] = hidden
+                sums[side].append(to_tile(hidden))
+        norm_store(sums, 1, 0)
         normed = u_scr[...]
-        key = dot(qkv_w[width:2 * width], normed).astype(bf16)
-        query = dot(qkv_w[:width], normed).astype(bf16)
+        pairs = heads // 2
+
+        def project_in(kind, lo, hi):
+            start = kind * width
+            return dot(qkv_w[start + lo * head_dim:start + hi * head_dim], normed).astype(bf16)
+
+        def per_head(rows):
+            return [rows[lo:lo + head_dim] for lo in range(0, rows.shape[0], head_dim)]
+
+        groups = ((0, 2), (2, heads))
+        keys, queries = [], []
+        for lo, hi in groups:
+            keys += per_head(project_in(1, lo, hi))
+            queries += per_head(project_in(0, lo, hi))
+        for (pair, part), both in fills.items():
+            store_fill(pair, part, both)
         factor = LOG2E * head_dim ** -0.5
 
-        def head(rows, index):
-            return rows[index * head_dim:(index + 1) * head_dim]
-
         def score(index):
-            return dot(head(key, index).T, head(query, index))
+            return [dot(keys[head].T, queries[head]) for head in (2 * index, 2 * index + 1)]
 
         def softmax(scores):
             top = jnp.max(scores, axis=0, keepdims=True)
             expo = jnp.exp2((scores - top) * factor)
             return expo.astype(bf16), 1.0 / fold(expo)
 
-        scores = {0: score(0), 1: score(1)}
-        value = dot(qkv_w[2 * width:], normed).astype(bf16)
-        fills = [(pair, part) for pair in (1, 2) for part in range(parts)]
-        split = 256 // head_dim
+        scores = [score(0)]
+        values = per_head(project_in(2, 0, heads // 2)) + per_head(project_in(2, heads // 2, heads))
         proj = [None, None]
-        mid = width // 2
-
-        def project(lo, hi):
-            rows = o_scr[lo:hi]
+
+        def project_out(lo, hi):
             for side in range(2):
-                piece = dot(proj_w[side * mid:side * mid + mid, lo:hi], rows)
+                piece = dot(proj_w[side * quarter:side * quarter + quarter, lo:hi], o_scr[lo:hi])
                 proj[side] = piece if proj[side] is None else proj[side] + piece
 
-        for index in range(heads):
-            if index + 2 < heads:
-                scores[index + 2] = score(index + 2)
-            cur = scores.pop(index)
-            done = [softmax(cur[:, half]) for half in halves]
-            expo = jnp.concatenate([pair[0] for pair in done], axis=1)
-            inverse = jnp.concatenate([pair[1] for pair in done], axis=1)
-            o_scr[index * head_dim:(index + 1) * head_dim] = (dot(head(value, index), expo) * inverse).astype(bf16)
-            if index < len(fills):
-                fill_lanes(step, *fills[index])
+        for index in range(pairs):
+            if index + 1 < pairs:
+                scores.append(score(index + 1))
+            for unit in range(2):
+                head = 2 * index + unit
+                done = [softmax(scores[index][unit][:, half]) for half in halves]
+                inverse = jnp.concatenate([pair[1] for pair in done], axis=1)
+                expo = jnp.concatenate([pair[0] for pair in done], axis=1)
+                o_scr[head * head_dim:(head + 1) * head_dim] = (dot(values[head], expo) * inverse).astype(bf16)
             if index == 0:
                 beside()
-            if index == split - 1:
-                project(0, 256)
-        project(256, width)
-        for half in halves:
-            hidden = hidden_in(half) + lanes[2] * jnp.concatenate([side[:, half] for side in proj], axis=0)
-            h_scr[:, half] = hidden
-            norm_into(hidden, 4, 3, half)
+            if index == 1:
+                project_out(0, 256)
+        project_out(256, width)
+        sums = [[], []]
+        for unit in range(2):
+            for part in range(each):
+                lo = unit * quarter + part * UNIT
+                rows = slice(lo, lo + UNIT)
+                piece = proj[unit][part * UNIT:part * UNIT + UNIT]
+                for side, half in enumerate(halves):
+                    hidden = h_scr[rows, half] + lanes[2, rows] * piece[:, half]
+                    h_scr[rows, half] = hidden
+                    sums[side].append(to_tile(hidden))
+        norm_store(sums, 4, 3)
         normed = u_scr[...]
-        count = mlp // CHUNK
-        ups = {}
-
-        def up(index):
-            return dot(up_w[index * CHUNK:(index + 1) * CHUNK], normed)
-
-        ups[0] = up(0)
-        total = [None, None]
-        for index in range(count):
-            if index + 1 < count:
-                ups[index + 1] = up(index + 1)
-            pre = ups.pop(index)
-            act = (pre * jnp.tanh(pre * (2.0 * GELU_A + 8.0 * GELU_B * (pre * pre))) + pre).astype(bf16)
+        tile_count = mlp // 256
+        ups = [dot(up_w[tile * 256:tile * 256 + 256], normed) for tile in range(tile_count)]
+
+        def gelu(pre):
+            return (pre * jnp.tanh(pre * (2.0 * GELU_A + 8.0 * GELU_B * (pre * pre))) + pre).astype(bf16)
+
+        after = jnp.minimum(step + 1, steps - 1)
+        down = [None, None]
+        for tile in range(tile_count):
+            act = jnp.concatenate([gelu(ups[tile][lo:lo + UNIT]) for lo in range(0, 256, UNIT)], axis=0)
+            if tile == tile_count - 1:
+                for part in range(parts):
+                    store_fill(0, part, fill(after, 0, part))
             for side in range(2):
-                piece = dot(down_w[side * mid:side * mid + mid, index * CHUNK:(index + 1) * CHUNK], act)
-                total[side] = piece if total[side] is None else total[side] + piece
-        for half in halves:
-            yield half, h_scr[:, half] + lanes[5] * jnp.concatenate([side[:, half] for side in total], axis=0)
+                piece = dot(down_w[side * quarter:side * quarter + quarter, tile * 256:tile * 256 + 256], act)
+                down[side] = piece if down[side] is None else down[side] + piece
+        for unit in range(2):
+            for part in range(each):
+                lo = unit * quarter + part * UNIT
+                rows = slice(lo, lo + UNIT)
+                for half in halves:
+                    yield rows, half, h_scr[rows, half] + lanes[5, rows] * down[unit][part * UNIT:part * UNIT + UNIT, half]
 
     def send(step, columns):
-        for half, hidden in columns:
-            sent[step, :, half] = hidden.astype(bf16)
+        for rows, half, hidden in columns:
+            sent[step, rows, half] = hidden.astype(bf16)
         hidden_copy(step).start()
 
     def received(step):
-        return lambda half: recv[step, :, half].astype(f32)
+        return lambda half, rows=slice(None): recv[step, rows, half].astype(f32)
 
     def wait_hidden(step):
         @pl.when(step >= 2)
@@ -220,9 +312,8 @@
         @pl.when(step >= 2)
         def _():
             latent_copy(step - 2).wait_recv()
-        embedded = dot(w_in_t[...], x_recv[step].astype(bf16))
-        h_last[...] = embedded
-        send(step, block(step, lambda half: h_last[:, half]))
+        h_last[...] = dot(w_in_t[...], x_recv[step].astype(bf16))
+        send(step, block(step, lambda half, rows=slice(None): h_last[rows, half]))
         return carry
 
     def middle_step(step, carry):
@@ -246,8 +337,8 @@
             x_cur[...] = x_next
             x_recv[jnp.minimum(before + 2, steps - 1)] = x_next
 
-        for half, hidden in block(step, received(step), beside):
-            h_last[:, half] = hidden
+        for rows, half, hidden in block(step, received(step), beside):
+            h_last[rows, half] = hidden
 
         @pl.when((step > 0) & (before + 2 < first_trips))
         def _():
@@ -300,7 +391,6 @@
         width, mlp = w_up.shape[1], w_up.shape[2]
         heads, head_dim = w_proj.shape[1], w_proj.shape[2]
         mod_rows = mod_table.shape[2] * width // 128
-        lanes_k = 3 * (mod_rows + -mod_rows % 8)
         bf16, f32 = jnp.bfloat16, jnp.float32
         vmem = pl.BlockSpec(memory_space=pltpu.VMEM)
         smem = pl.BlockSpec(memory_space=pltpu.SMEM)
@@ -321,8 +411,8 @@
                 pltpu.VMEM((width, width), bf16),
                 pltpu.VMEM((mlp, width), bf16),
                 pltpu.VMEM((width, mlp), bf16),
-                pltpu.VMEM((steps, 128, lanes_k), bf16),
-                pltpu.VMEM((3 * width // 128, lanes_k, 256), bf16),
+                pltpu.VMEM((steps, 128, 128), bf16),
+                pltpu.VMEM((3 * width // 128, 128, 256), bf16),
                 pltpu.VMEM((6, width, 128), f32),
                 pltpu.VMEM((steps, width, tokens), bf16),
                 pltpu.VMEM((steps, width, tokens), bf16),

time: 112 us -> 102 us (0.911)
  Pallas kernels: 110 us -> 100 us
    pallas_call x1, Pallas kernels: 110 us -> 100 us  [shard_body(): pl.pallas_call(functools.partial(kernel, stages), out_shape=jax.ShapeDtyp...]
where the time goes in v3:
time: 102 us
  Pallas kernels  100 us (98%)
  local copies, waits for them, and re-layouts  1.32 us (1%)
    pallas_call x1, Pallas kernels, shard_body(): pl.pallas_call(functools.partial(kernel, stages), out_shape=jax.ShapeDtyp...  100 us

profile of v3, /device:TPU:81, one launch (start us, length us, event | category | flops | bytes accessed | tf_op | source)
XLA Modules:
  0.0 101.8 jit_solution(4631782389223673172)
XLA Ops:
  0.0 100.5 %stage_loop.1 = f32[16,256]{1,0:T(8,128)} custom-call(f32[16,256]{1,0:T(8,128)} %bitcast.18, bf16[16,384]{1,0:T(8,128)(2,1)} %w_in_ref.1, bf16[16,384]{1,0:T(8,128)(2,1)} %bitcast.19, bf16[384,1152]{1,0:T(8,128)(2,1)} %bitcast.14, bf16[6,64,384]{2,1,0:T(8,128)(2,1)} %bitcast.15, bf16[384,1536]{1,0:T(8,128)(2,1)} %bitcast.12, bf16[1536,384]{1,0:T(8,128)(2,1)} %bitcast.13, ...), custom_call_target="tpu_custom_call" | custom-call | tf_op jit(solution)/shard_map/stage_loop/pallas_call | solution.py:398
  100.5 1.3 %copy.13 = f32[1,256,16]{1,2,0:T(8,128)} copy(f32[1,256,16]{1,2,0:T(8,128)} %bitcast.17) | data formatting | bytes 32768

commit v4 on v3

--- a/solution.py
+++ b/solution.py
@@ -37,9 +37,9 @@
     return jnp.dot(lhs, rhs, preferred_element_type=jnp.float32)
 
 
-def kernel(stages, x_ref, w_in_ref, w_out_ref, qkv_hbm, proj_hbm, up_hbm, down_hbm, mod_ref, keep_ref, noise_ref, warm_hbm,
-           out_ref, qkv_n, proj_n, up_n, down_n, warm_n, w_in_t, qkv_w, proj_w, up_w, down_w, mod_s, select, lanes,
-           recv, sent, x_recv, x_cur, h_last, h_scr, u_scr, o_scr, load_sem, recv_sem, send_sem, x_recv_sem, x_send_sem, last_send_sem, last_recv_sem):
+def kernel(stages, x_hbm, w_in_hbm, w_out_hbm, qkv_hbm, proj_hbm, up_hbm, down_hbm, mod_hbm, keep_ref, noise_ref, warm_hbm,
+           out_ref, x_ref, w_in_ref, w_out_ref, mod_ref, qkv_n, proj_n, up_n, down_n, warm_n, w_in_t, qkv_w, proj_w, up_w, down_w, mod_s, select, lanes,
+           recv, sent, x_recv, x_cur, h_last, h_scr, u_scr, o_scr, p_scr, load_sem, recv_sem, send_sem, x_recv_sem, x_send_sem, last_send_sem, last_recv_sem):
     stage = lax.axis_index('stage')
     is_first = stage == 0
     is_last = stage == stages - 1
@@ -55,13 +55,18 @@
         pltpu.make_async_copy(proj_hbm, proj_n, load_sem.at[2]),
         pltpu.make_async_copy(up_hbm, up_n, load_sem.at[3]),
         pltpu.make_async_copy(down_hbm, down_n, load_sem.at[4]),
+        pltpu.make_async_copy(x_hbm, x_ref, load_sem.at[5]),
+        pltpu.make_async_copy(w_in_hbm, w_in_ref, load_sem.at[6]),
+        pltpu.make_async_copy(w_out_hbm, w_out_ref, load_sem.at[7]),
+        pltpu.make_async_copy(mod_hbm, mod_ref, load_sem.at[8]),
     ]
-    for copy in loads:
-        copy.start()
+    for index in (8, 5, 6, 7, 0, 1, 2, 3, 4):
+        loads[index].start()
     barrier = pltpu.get_barrier_semaphore()
     for ahead in range(1, stages):
         pl.semaphore_signal(barrier, inc=1, device_id={'stage': lax.rem(stage + ahead, stages)}, device_id_type=MESH)
 
+    loads[8].wait()
     mod_rows = mod_ref.shape[0] // steps
     parts = width // 128
     pad = mod_rows + -mod_rows % 8
@@ -71,16 +76,14 @@
     gap = jnp.zeros((pad - mod_rows, 128), f32)
     rest_rows = jnp.zeros((128 - 3 * pad, 128), f32)
 
-    def split_mod(step, carry):
-        rows = mod_ref[pl.ds(step * mod_rows, mod_rows)] + plus
+    for step in range(steps):
+        rows = mod_ref[step * mod_rows:(step + 1) * mod_rows] + plus
         high = jnp.clip(rows, -limit, limit).astype(bf16).astype(f32)
         rest = rows - high
         mid = rest.astype(bf16).astype(f32)
         terms = jnp.concatenate([high, gap, mid, gap, rest - mid, gap, rest_rows], axis=0)
         mod_s[step] = terms.T.astype(bf16)
-        return carry
-
-    lax.fori_loop(0, steps, split_mod, 0)
+
     term = lax.broadcasted_iota(jnp.int32, (128, 256), 0)
     term = jnp.where(term < 3 * pad, term % pad, -1)
     column = lax.broadcasted_iota(jnp.int32, (128, 256), 1) // 128
@@ -98,6 +101,8 @@
 
     halves = [slice(lo, lo + 128) for lo in range(0, tokens, 128)]
 
+    for index in (5, 6, 7):
+        loads[index].wait()
     w_in_t[...] = w_in_ref[...].T
     x_cur[...] = x_ref[...]
     for slot in range(2):
@@ -239,33 +244,39 @@
 
         scores = [score(0)]
         values = per_head(project_in(2, 0, heads // 2)) + per_head(project_in(2, heads // 2, heads))
+        beside()
         proj = [None, None]
 
         def project_out(lo, hi):
             for side in range(2):
                 piece = dot(proj_w[side * quarter:side * quarter + quarter, lo:hi], o_scr[lo:hi])
-                proj[side] = piece if proj[side] is None else proj[side] + piece
+                if lo == 0:
+                    p_scr[side * quarter:side * quarter + quarter] = piece
+                else:
+                    proj[side] = piece
 
         for index in range(pairs):
             if index + 1 < pairs:
                 scores.append(score(index + 1))
+            outs = []
             for unit in range(2):
                 head = 2 * index + unit
                 done = [softmax(scores[index][unit][:, half]) for half in halves]
                 inverse = jnp.concatenate([pair[1] for pair in done], axis=1)
                 expo = jnp.concatenate([pair[0] for pair in done], axis=1)
-                o_scr[head * head_dim:(head + 1) * head_dim] = (dot(values[head], expo) * inverse).astype(bf16)
-            if index == 0:
-                beside()
-            if index == 1:
+                outs.append((dot(values[head], expo), inverse))
+            if index == pairs - 1:
                 project_out(0, 256)
+            for unit, (out, inverse) in enumerate(outs):
+                head = 2 * index + unit
+                o_scr[head * head_dim:(head + 1) * head_dim] = (out * inverse).astype(bf16)
         project_out(256, width)
         sums = [[], []]
         for unit in range(2):
             for part in range(each):
                 lo = unit * quarter + part * UNIT
                 rows = slice(lo, lo + UNIT)
-                piece = proj[unit][part * UNIT:part * UNIT + UNIT]
+                piece = proj[unit][part * UNIT:part * UNIT + UNIT] + p_scr[rows]
                 for side, half in enumerate(halves):
                     hidden = h_scr[rows, half] + lanes[2, rows] * piece[:, half]
                     h_scr[rows, half] = hidden
@@ -398,9 +409,13 @@
         out = pl.pallas_call(
             functools.partial(kernel, stages),
             out_shape=jax.ShapeDtypeStruct((chan, tokens), f32),
-            in_specs=[vmem, vmem, vmem, hbm, hbm, hbm, hbm, vmem, smem, smem, hbm],
+            in_specs=[hbm] * 8 + [smem, smem, hbm],
             out_specs=vmem,
             scratch_shapes=[
+                pltpu.VMEM((chan, tokens), f32),
+                pltpu.VMEM((chan, width), bf16),
+                pltpu.VMEM((chan, width), bf16),
+                pltpu.VMEM((steps * mod_rows, 128), f32),
                 pltpu.VMEM((width, 3 * width), bf16),
                 pltpu.VMEM((heads, head_dim, width), bf16),
                 pltpu.VMEM((width, mlp), bf16),
@@ -422,7 +437,8 @@
                 pltpu.VMEM((width, tokens), f32),
                 pltpu.VMEM((width, tokens), bf16),
                 pltpu.VMEM((width, tokens), bf16),
-                pltpu.SemaphoreType.DMA((5,)),
+                pltpu.VMEM((width, tokens), f32),
+                pltpu.SemaphoreType.DMA((9,)),
                 pltpu.SemaphoreType.DMA((steps,)),
                 pltpu.SemaphoreType.DMA((steps,)),
                 pltpu.SemaphoreType.DMA((steps,)),

time: 102 us -> 98.4 us (0.965)
  Pallas kernels: 100 us -> 96.8 us
    pallas_call x1, Pallas kernels: 100 us -> 96.8 us  [shard_body(): pl.pallas_call(functools.partial(kernel, stages), out_shape=jax.ShapeDtyp...]
where the time goes in v4:
time: 98.4 us; the launch traced here: 98.2 us
  Pallas kernels  96.8 us (98%)
  local copies, waits for them, and re-layouts  1.32 us (1%)
    pallas_call x1, Pallas kernels, shard_body(): pl.pallas_call(functools.partial(kernel, stages), out_shape=jax.ShapeDtyp...  96.8 us

profile of v4, /device:TPU:81, one launch (start us, length us, event | category | flops | bytes accessed | tf_op | source)
XLA Modules:
  0.0 98.2 jit_solution(5137492880694448406)
XLA Ops:
  0.0 96.8 %stage_loop.1 = f32[16,256]{1,0:T(8,128)} custom-call(f32[16,256]{1,0:T(8,128)} %bitcast.18, bf16[16,384]{1,0:T(8,128)(2,1)} %w_in_hbm.1, bf16[16,384]{1,0:T(8,128)(2,1)} %bitcast.19, bf16[384,1152]{1,0:T(8,128)(2,1)} %bitcast.14, bf16[6,64,384]{2,1,0:T(8,128)(2,1)} %bitcast.15, bf16[384,1536]{1,0:T(8,128)(2,1)} %bitcast.12, bf16[1536,384]{1,0:T(8,128)(2,1)} %bitcast.13, ...), custom_call_target="tpu_custom_call" | custom-call | tf_op jit(solution)/shard_map/stage_loop/pallas_call | solution.py:409
  96.8 1.3 %copy.13 = f32[1,256,16]{1,2,0:T(8,128)} copy(f32[1,256,16]{1,2,0:T(8,128)} %bitcast.17) | data formatting | bytes 32768

commit v5 on v4

--- a/solution.py
+++ b/solution.py
@@ -242,9 +242,11 @@
             expo = jnp.exp2((scores - top) * factor)
             return expo.astype(bf16), 1.0 / fold(expo)
 
+        beside()
         scores = [score(0)]
-        values = per_head(project_in(2, 0, heads // 2)) + per_head(project_in(2, heads // 2, heads))
-        beside()
+        values = per_head(project_in(2, 0, 2))
+        scores.append(score(1))
+        values += per_head(project_in(2, 2, heads))
         proj = [None, None]
 
         def project_out(lo, hi):
@@ -256,8 +258,8 @@
                     proj[side] = piece
 
         for index in range(pairs):
-            if index + 1 < pairs:
-                scores.append(score(index + 1))
+            if index + 2 < pairs:
+                scores.append(score(index + 2))
             outs = []
             for unit in range(2):
                 head = 2 * index + unit
@@ -267,6 +269,9 @@
                 outs.append((dot(values[head], expo), inverse))
             if index == pairs - 1:
                 project_out(0, 256)
+                after = jnp.minimum(step + 1, steps - 1)
+                for part in range(parts):
+                    store_fill(0, part, fill(after, 0, part))
             for unit, (out, inverse) in enumerate(outs):
                 head = 2 * index + unit
                 o_scr[head * head_dim:(head + 1) * head_dim] = (out * inverse).astype(bf16)
@@ -289,13 +294,9 @@
         def gelu(pre):
             return (pre * jnp.tanh(pre * (2.0 * GELU_A + 8.0 * GELU_B * (pre * pre))) + pre).astype(bf16)
 
-        after = jnp.minimum(step + 1, steps - 1)
         down = [None, None]
         for tile in range(tile_count):
             act = jnp.concatenate([gelu(ups[tile][lo:lo + UNIT]) for lo in range(0, 256, UNIT)], axis=0)
-            if tile == tile_count - 1:
-                for part in range(parts):
-                    store_fill(0, part, fill(after, 0, part))
             for side in range(2):
                 piece = dot(down_w[side * quarter:side * quarter + quarter, tile * 256:tile * 256 + 256], act)
                 down[side] = piece if down[side] is None else down[side] + piece

time: 98.4 us -> 96.8 us (0.984)
  Pallas kernels: 96.8 us -> 95.3 us
    pallas_call x1, Pallas kernels: 96.8 us -> 95.3 us  [shard_body(): pl.pallas_call(functools.partial(kernel, stages), out_shape=jax.ShapeDtyp...]
where the time goes in v5:
time: 96.8 us; the launch traced here: 96.6 us
  Pallas kernels  95.3 us (98%)
  local copies, waits for them, and re-layouts  1.32 us (1%)
    pallas_call x1, Pallas kernels, shard_body(): pl.pallas_call(functools.partial(kernel, stages), out_shape=jax.ShapeDtyp...  95.3 us

profile of v5, /device:TPU:81, one launch (start us, length us, event | category | flops | bytes accessed | tf_op | source)
XLA Modules:
  0.0 96.6 jit_solution(17403222514307453975)
XLA Ops:
  0.0 95.3 %stage_loop.1 = f32[16,256]{1,0:T(8,128)} custom-call(f32[16,256]{1,0:T(8,128)} %bitcast.18, bf16[16,384]{1,0:T(8,128)(2,1)} %w_in_hbm.1, bf16[16,384]{1,0:T(8,128)(2,1)} %bitcast.19, bf16[384,1152]{1,0:T(8,128)(2,1)} %bitcast.14, bf16[6,64,384]{2,1,0:T(8,128)(2,1)} %bitcast.15, bf16[384,1536]{1,0:T(8,128)(2,1)} %bitcast.12, bf16[1536,384]{1,0:T(8,128)(2,1)} %bitcast.13, ...), custom_call_target="tpu_custom_call" | custom-call | tf_op jit(solution)/shard_map/stage_loop/pallas_call | solution.py:410
  95.3 1.3 %copy.13 = f32[1,256,16]{1,2,0:T(8,128)} copy(f32[1,256,16]{1,2,0:T(8,128)} %bitcast.17) | data formatting | bytes 32768

commit v6 on v5

--- a/solution.py
+++ b/solution.py
@@ -105,18 +105,15 @@
         loads[index].wait()
     w_in_t[...] = w_in_ref[...].T
     x_cur[...] = x_ref[...]
-    for slot in range(2):
-        x_recv[slot] = x_ref[...]
-    loads[0].wait()
+    x_recv[0] = x_ref[...]
+    for index in range(5):
+        loads[index].wait()
     for slot in range(2):
         recv[slot] = warm_n[slot].T
-    loads[1].wait()
-    qkv_w[...] = qkv_n[...].T
-    loads[2].wait()
+    qkv_w[:2 * width] = qkv_n[:, :2 * width].T
+    qkv_w[2 * width:] = qkv_n[:, 2 * width:].T * jnp.asarray(1.0 / tokens, bf16)
     proj_w[...] = proj_n[...].reshape(width, width).T
-    loads[3].wait()
     up_w[...] = up_n[...].T * jnp.asarray(0.5, bf16)
-    loads[4].wait()
     down_w[...] = down_n[...].T
     for part in range(parts):
         store_fill(0, part, fill(0, 0, part))
@@ -131,7 +128,7 @@
 
     def latent_copy(step):
         return pltpu.make_async_remote_copy(
-            src_ref=x_recv.at[step + 2], dst_ref=x_recv.at[step + 2], send_sem=x_send_sem.at[step], recv_sem=x_recv_sem.at[step + 2],
+            src_ref=x_recv.at[step + 1], dst_ref=x_recv.at[step + 1], send_sem=x_send_sem.at[step], recv_sem=x_recv_sem.at[step],
             device_id=next_id, device_id_type=MESH)
 
     first_trips = steps - 2 * (stages - 1)
@@ -206,7 +203,7 @@
         lo = 0 if register == 0 else width - 256
         return ref[row:row + UNIT, lo:lo + 256]
 
-    def block(step, hidden_in, beside=lambda: None):
+    def block(step, hidden_in, beside=lambda: None, post=lambda: None):
         fills = {(pair, part): fill(step, pair, part) for pair in (1, 2) for part in range(parts)}
         sums = [[], []]
         for rows in row_units:
@@ -240,7 +237,7 @@
         def softmax(scores):
             top = jnp.max(scores, axis=0, keepdims=True)
             expo = jnp.exp2((scores - top) * factor)
-            return expo.astype(bf16), 1.0 / fold(expo)
+            return expo.astype(bf16), float(tokens) / fold(expo)
 
         beside()
         scores = [score(0)]
@@ -276,6 +273,7 @@
                 head = 2 * index + unit
                 o_scr[head * head_dim:(head + 1) * head_dim] = (out * inverse).astype(bf16)
         project_out(256, width)
+        post()
         sums = [[], []]
         for unit in range(2):
             for part in range(each):
@@ -321,9 +319,9 @@
             hidden_copy(step - 2).wait_recv()
 
     def first_step(step, carry):
-        @pl.when(step >= 2)
+        @pl.when(step >= 1)
         def _():
-            latent_copy(step - 2).wait_recv()
+            latent_copy(step - 1).wait_recv()
         h_last[...] = dot(w_in_t[...], x_recv[step].astype(bf16))
         send(step, block(step, lambda half, rows=slice(None): h_last[rows, half]))
         return carry
@@ -340,21 +338,22 @@
         x_cur[...] = x_next
         return x_next
 
-    def last_step(step, carry):
+    def last_step(sends, step, carry):
         wait_hidden(step)
         before = jnp.maximum(step - 1, 0)
 
         def beside():
             x_next = jnp.where(step > 0, advance(before), x_ref[...])
             x_cur[...] = x_next
-            x_recv[jnp.minimum(before + 2, steps - 1)] = x_next
-
-        for rows, half, hidden in block(step, received(step), beside):
+            if sends:
+                x_recv[step + 1] = x_next
+
+        def post():
+            if sends:
+                latent_copy(step).start()
+
+        for rows, half, hidden in block(step, received(step), beside, post):
             h_last[rows, half] = hidden
-
-        @pl.when((step > 0) & (before + 2 < first_trips))
-        def _():
-            latent_copy(before).start()
         return carry
 
     def final_copy(ahead):
@@ -373,9 +372,10 @@
     @pl.when(is_last)
     def _():
         h_last[...] = jnp.zeros_like(h_last)
-        lax.fori_loop(0, steps, last_step, 0)
+        lax.fori_loop(0, first_trips - 1, functools.partial(last_step, True), 0)
+        lax.fori_loop(first_trips - 1, steps, functools.partial(last_step, False), 0)
         out_ref[...] = advance(steps - 1)
-        for ahead in range(1, stages):
+        for ahead in sorted(range(1, stages), key=lambda ahead: -min(ahead, stages - ahead)):
             final_copy(ahead).start()
         for ahead in range(1, stages):
             final_copy(ahead).wait_send()
@@ -383,7 +383,7 @@
         def drain(step, carry):
             latent_copy(step).wait_send()
             return carry
-        lax.fori_loop(0, first_trips - 2, drain, 0)
+        lax.fori_loop(0, first_trips - 1, drain, 0)
 
     @pl.when(jnp.logical_not(is_last))
     def _():

time: 96.8 us -> 95.1 us (0.982)
  Pallas kernels: 95.3 us -> 93.5 us
    pallas_call x1, Pallas kernels: 95.3 us -> 93.5 us  [shard_body(): pl.pallas_call(functools.partial(kernel, stages), out_shape=jax.ShapeDtyp...]
where the time goes in v6:
time: 95.1 us; the launch traced here: 94.9 us
  Pallas kernels  93.5 us (98%)
  local copies, waits for them, and re-layouts  1.32 us (1%)
    pallas_call x1, Pallas kernels, shard_body(): pl.pallas_call(functools.partial(kernel, stages), out_shape=jax.ShapeDtyp...  93.5 us

profile of v6, /device:TPU:81, one launch (start us, length us, event | category | flops | bytes accessed | tf_op | source)
XLA Modules:
  0.0 94.9 jit_solution(13462876232396701996)
XLA Ops:
  0.0 93.5 %stage_loop.1 = f32[16,256]{1,0:T(8,128)} custom-call(f32[16,256]{1,0:T(8,128)} %bitcast.18, bf16[16,384]{1,0:T(8,128)(2,1)} %w_in_hbm.1, bf16[16,384]{1,0:T(8,128)(2,1)} %bitcast.19, bf16[384,1152]{1,0:T(8,128)(2,1)} %bitcast.14, bf16[6,64,384]{2,1,0:T(8,128)(2,1)} %bitcast.15, bf16[384,1536]{1,0:T(8,128)(2,1)} %bitcast.12, bf16[1536,384]{1,0:T(8,128)(2,1)} %bitcast.13, ...), custom_call_target="tpu_custom_call" | custom-call | tf_op jit(solution)/shard_map/stage_loop/pallas_call | solution.py:410
  93.5 1.3 %copy.13 = f32[1,256,16]{1,2,0:T(8,128)} copy(f32[1,256,16]{1,2,0:T(8,128)} %bitcast.17) | data formatting | bytes 32768

commit v7 on v6

--- a/solution.py
+++ b/solution.py
@@ -12,7 +12,7 @@
 LOG2E = math.log2(math.e)
 GELU_A = math.sqrt(2.0 / math.pi)
 GELU_B = GELU_A * 0.044715
-UNIT = 64
+UNIT = 32
 MESH = pl.DeviceIdType.MESH
 
 
@@ -235,9 +235,12 @@
             return [dot(keys[head].T, queries[head]) for head in (2 * index, 2 * index + 1)]
 
         def softmax(scores):
-            top = jnp.max(scores, axis=0, keepdims=True)
+            best = scores
+            while best.shape[0] > 8:
+                best = jnp.maximum(best[:best.shape[0] // 2], best[best.shape[0] // 2:])
+            top = jnp.max(best, axis=0, keepdims=True)
             expo = jnp.exp2((scores - top) * factor)
-            return expo.astype(bf16), float(tokens) / fold(expo)
+            return expo.astype(bf16), float(tokens) / jnp.sum(expo, axis=0, keepdims=True)
 
         beside()
         scores = [score(0)]
@@ -275,8 +278,8 @@
         project_out(256, width)
         post()
         sums = [[], []]
-        for unit in range(2):
-            for part in range(each):
+        for part in range(each):
+            for unit in range(2):
                 lo = unit * quarter + part * UNIT
                 rows = slice(lo, lo + UNIT)
                 piece = proj[unit][part * UNIT:part * UNIT + UNIT] + p_scr[rows]

time: 95.1 us -> 94.6 us (level)
  no operation moved by 1% of the time
where the time goes in v7:
time: 94.6 us; the launch traced here: 94.4 us
  Pallas kernels  93.1 us (98%)
  local copies, waits for them, and re-layouts  1.32 us (1%)
    pallas_call x1, Pallas kernels, shard_body(): pl.pallas_call(functools.partial(kernel, stages), out_shape=jax.ShapeDtyp...  93.1 us

profile of v7, /device:TPU:81, one launch (start us, length us, event | category | flops | bytes accessed | tf_op | source)
XLA Modules:
  0.0 94.4 jit_solution(16046074921079002904)
XLA Ops:
  0.0 93.1 %stage_loop.1 = f32[16,256]{1,0:T(8,128)} custom-call(f32[16,256]{1,0:T(8,128)} %bitcast.18, bf16[16,384]{1,0:T(8,128)(2,1)} %w_in_hbm.1, bf16[16,384]{1,0:T(8,128)(2,1)} %bitcast.19, bf16[384,1152]{1,0:T(8,128)(2,1)} %bitcast.14, bf16[6,64,384]{2,1,0:T(8,128)(2,1)} %bitcast.15, bf16[384,1536]{1,0:T(8,128)(2,1)} %bitcast.12, bf16[1536,384]{1,0:T(8,128)(2,1)} %bitcast.13, ...), custom_call_target="tpu_custom_call" | custom-call | tf_op jit(solution)/shard_map/stage_loop/pallas_call | solution.py:413
  93.1 1.3 %copy.13 = f32[1,256,16]{1,2,0:T(8,128)} copy(f32[1,256,16]{1,2,0:T(8,128)} %bitcast.17) | data formatting | bytes 32768

commit v8 on v7

--- a/solution.py
+++ b/solution.py
@@ -244,9 +244,9 @@
 
         beside()
         scores = [score(0)]
-        values = per_head(project_in(2, 0, 2))
+        values = per_head(project_in(2, 0, 4))
         scores.append(score(1))
-        values += per_head(project_in(2, 2, heads))
+        values += per_head(project_in(2, 4, heads))
         proj = [None, None]
 
         def project_out(lo, hi):

time: 94.6 us -> 94.8 us (level)
  no operation moved by 1% of the time
where the time goes in v8:
time: 94.8 us; the launch traced here: 94.6 us
  Pallas kernels  93.3 us (98%)
  local copies, waits for them, and re-layouts  1.32 us (1%)
    pallas_call x1, Pallas kernels, shard_body(): pl.pallas_call(functools.partial(kernel, stages), out_shape=jax.ShapeDtyp...  93.3 us

profile of v8, /device:TPU:81, one launch (start us, length us, event | category | flops | bytes accessed | tf_op | source)
XLA Modules:
  0.0 94.6 jit_solution(7959553504598300152)
XLA Ops:
  0.0 93.3 %stage_loop.1 = f32[16,256]{1,0:T(8,128)} custom-call(f32[16,256]{1,0:T(8,128)} %bitcast.18, bf16[16,384]{1,0:T(8,128)(2,1)} %w_in_hbm.1, bf16[16,384]{1,0:T(8,128)(2,1)} %bitcast.19, bf16[384,1152]{1,0:T(8,128)(2,1)} %bitcast.14, bf16[6,64,384]{2,1,0:T(8,128)(2,1)} %bitcast.15, bf16[384,1536]{1,0:T(8,128)(2,1)} %bitcast.12, bf16[1536,384]{1,0:T(8,128)(2,1)} %bitcast.13, ...), custom_call_target="tpu_custom_call" | custom-call | tf_op jit(solution)/shard_map/stage_loop/pallas_call | solution.py:413
  93.3 1.3 %copy.13 = f32[1,256,16]{1,2,0:T(8,128)} copy(f32[1,256,16]{1,2,0:T(8,128)} %bitcast.17) | data formatting | bytes 32768
